TPU v7x, 32 devices: a whole 2x2x4 slice. The times are simulated.
32 devices in a mesh: site: 8 (over z, x), dom: 4 (over y, core).
Axes of the slice: x: 2, y: 2, z: 4, core: 2. Of those that a mesh axis runs over, the one named last changes fastest.
Arguments:
- top_partial: float32 [16, 61, 4, 8192], P(None, None, 'dom', 'site'), may hold values from 0.001 to 1
- bottom_partial: float32 [16, 61, 4, 8192], P(None, None, 'dom', 'site'), may hold values from 0.001 to 1
- left_vectors: float32 [256, 61, 61], P('dom'), may hold values from 0.05 to 1
- right_vectors: float32 [256, 61, 61], P('dom'), may hold values from 0.05 to 1
- decay_rates: float32 [256, 61], P('dom'), may hold values from 0.05 to 8
- state_weights: float32 [256, 61], P('dom'), may hold values from 0.002 to 0.05
- part_rates: float32 [256], P('dom'), may hold values from 0.3 to 3
- branch_lengths: float32 [1997], replicated, may hold values from 0.02 to 0.5
- pattern_weights: int32 [4, 8192], P('dom', 'site'), may hold values from 0 to 9
- block_partition: int32 [4, 64], P('dom', 'site'), may hold values from 0 to 255
- chosen_branches: int32 [16], replicated, may hold values from 0 to 1996, as said below
Outputs:
- site_loglik: float32 [16, 4, 8192], P(None, 'dom', 'site')
- part_derivs: float32 [2, 16, 256], P(None, None, 'dom')
- new_lengths: float32 [1997], replicated
Inputs may be any that keep to these rules, and one draw needn't show every extreme that they name: `chosen_branches`: distinct branch numbers.
All inputs are finite; a program needn't handle non-finite values.
Results may differ from a plain program's by a relative error of at most 0.0003.
Values sent between devices are 32-bit elements; how exact they have to be, the bound alone decides.
A program may use at most 64 MiB of HBM per device.

v0:
```python
import jax
import jax.numpy as jnp
from jax import lax
from jax.sharding import PartitionSpec as P

BLK = 128


def project(upper, lower, vec_left, vec_right, state_w):
    scaled = upper * jnp.transpose(state_w)[None, :, :, None]
    lefts = jnp.einsum("binl,nik->bknl", scaled, vec_left, precision=lax.Precision.HIGHEST)
    rights = jnp.einsum("nkj,bjnl->bknl", vec_right, lower, precision=lax.Precision.HIGHEST)
    return (lefts, rights)


def finish(lefts, rights, exponent, times, weight_f):
    joint = lefts * rights
    expo = jnp.transpose(exponent)[None, :, :, None]
    decayed = joint * jnp.exp(expo * times[:, None, None, None])
    like_zero = jnp.sum(decayed, axis=1)
    like_one = jnp.sum(decayed * expo, axis=1)
    like_two = jnp.sum(decayed * expo * expo, axis=1)
    first = like_one / like_zero
    second = like_two / like_zero - first * first
    loglik = weight_f[None] * jnp.log(like_zero)
    sums = jnp.stack(
        [jnp.sum(weight_f[None] * first, axis=-1), jnp.sum(weight_f[None] * second, axis=-1)]
    )
    return (loglik, sums)


def on_device(
    top_partial,
    bottom_partial,
    left_vectors,
    right_vectors,
    decay_rates,
    state_weights,
    part_rates,
    branch_lengths,
    pattern_weights,
    block_partition,
    chosen_branches,
):
    times = branch_lengths[chosen_branches]
    branches = top_partial.shape[0]
    states = top_partial.shape[1]
    sites_here = top_partial.shape[3]
    nblocks = sites_here // BLK
    upper = top_partial.reshape(branches, states, nblocks, BLK)
    lower = bottom_partial.reshape(branches, states, nblocks, BLK)
    blocks = block_partition[0]
    owned = left_vectors.shape[0]
    groups = lax.axis_size("dom")
    parts_all = owned * groups
    wanted = lax.all_gather(block_partition, "dom", axis=0, tiled=True)
    relative = wanted - lax.axis_index("dom") * owned
    inside = jnp.logical_and(relative >= 0, relative < owned).astype(jnp.float32)
    clipped = jnp.clip(relative, 0, owned - 1)
    send_left = left_vectors[clipped] * inside[:, :, None, None]
    send_right = right_vectors[clipped] * inside[:, :, None, None]
    send_decay = decay_rates[clipped] * inside[:, :, None]
    send_weight = state_weights[clipped] * inside[:, :, None]
    send_rate = part_rates[clipped] * inside
    received = (
        lax.all_to_all(send_left, "dom", split_axis=0, concat_axis=0, tiled=True),
        lax.all_to_all(send_right, "dom", split_axis=0, concat_axis=0, tiled=True),
        lax.all_to_all(send_decay, "dom", split_axis=0, concat_axis=0, tiled=True),
        lax.all_to_all(send_weight, "dom", split_axis=0, concat_axis=0, tiled=True),
        lax.all_to_all(send_rate, "dom", split_axis=0, concat_axis=0, tiled=True),
    )
    vec_left = jnp.sum(received[0], axis=0)
    vec_right = jnp.sum(received[1], axis=0)
    decay_b = jnp.sum(received[2], axis=0)
    weight_b = jnp.sum(received[3], axis=0)
    rate_b = jnp.sum(received[4], axis=0)
    exponent = -decay_b * rate_b[:, None]
    lefts, rights = project(upper, lower, vec_left, vec_right, weight_b)
    weight_f = pattern_weights[0].astype(jnp.float32).reshape(nblocks, BLK)
    loglik, sums = finish(lefts, rights, exponent, times, weight_f)
    onehot = (blocks[:, None] == jnp.arange(parts_all, dtype=jnp.int32)[None, :]).astype(
        jnp.float32
    )
    part_local = jnp.einsum("abn,np->abp", sums, onehot, precision=lax.Precision.HIGHEST)
    everything = lax.psum(part_local, ("site", "dom"))
    share = lax.dynamic_slice_in_dim(everything, lax.axis_index("dom") * owned, owned, 2)
    totals = jnp.sum(everything, axis=2)
    updated = times - totals[0] / totals[1]
    new_lengths = branch_lengths.at[chosen_branches].set(updated)
    return (loglik.reshape(branches, 1, sites_here), share, new_lengths)


def solution(mesh):
    return jax.shard_map(
        on_device,
        mesh=mesh,
        in_specs=(
            P(None, None, "dom", "site"),
            P(None, None, "dom", "site"),
            P("dom", None, None),
            P("dom", None, None),
            P("dom", None),
            P("dom", None),
            P("dom"),
            P(),
            P("dom", "site"),
            P("dom", "site"),
            P(),
        ),
        out_specs=(P(None, "dom", "site"), P(None, None, "dom"), P()),
        check_vma=False,
    )
```

profile of v0, /device:TPU:0, one launch (start us, length us, event | category | flops | bytes accessed | tf_op | source)
XLA Modules:
  0.0 121.8 jit_solution(4191838396032848199)
XLA Ops:
  0.6 0.8 copy.76
  1.5 6.2 %all-gather = s32[4,1,8]{2,1,0:T(1,128)S(1)} all-gather(s32[1,1,8]{2,1,0:T(1,128)} %bitcast.55), channel_id=1, replica_groups=mesh['site'=8,'dom'=4] {'dom'}, dimensions={0}, use_global_device_ids=true | all-gather | bytes 160 | tf_op jit(solution)/shard_map/all_gather | solution.py:56
  7.7 0.1 reshape.73
  7.8 1.4 %gather_fusion.4 = f32[32]{0:T(128)S(1)} fusion(f32[64]{0:T(128)} %param.17, s32[1024]{0:T(1024)S(1)} %pad_clamp_fusion.1), kind=kCustom, calls=%fused_computation.4 | custom fusion | bytes 384 | tf_op jit(solution)/shard_map/gather | solution.py:64
  9.2 0.1 reshape.104
  9.3 0.6 bitcast_select_fusion
  9.9 3.2 %all-to-all-start.4 = ((f32[4,1,8]{2,1,0:T(1,128)}), f32[4,1,8]{2,1,0:T(1,128)S(1)}, u32[]{:S(2)}, u32[]{:S(2)}) async-start(f32[4,1,8]{2,1,0:T(1,128)} %bitcast.14), calls=%async_computation.4 | async-start | bytes 4096 | tf_op jit(solution)/shard_map/all_to_all | solution.py:70
  13.1 1.3 %gather_fusion.3 = f32[32,61]{1,0:T(8,128)S(1)} fusion(f32[64,61]{1,0:T(8,128)} %param.15, s32[1024]{0:T(1024)S(1)} %pad_clamp_fusion.1), kind=kCustom, calls=%fused_computation.3 | custom fusion | bytes 15744 | tf_op jit(solution)/shard_map/gather | solution.py:62
  14.4 1.3 %gather_fusion.1 = f32[32,61]{1,0:T(8,128)S(1)} fusion(f32[64,61]{1,0:T(8,128)} %param.16, s32[1024]{0:T(1024)S(1)} %pad_clamp_fusion.1), kind=kCustom, calls=%fused_computation.1 | custom fusion | bytes 15744 | tf_op jit(solution)/shard_map/gather | solution.py:63
  15.8 0.1 bitcast_multiply_fusion.2
  15.8 0.7 reshape.156
  16.5 0.3 all-to-all-done.4
  16.8 3.2 %all-to-all-start.3 = ((f32[4,1,488]{2,1,0:T(1,128)}), f32[4,1,488]{2,1,0:T(1,128)S(1)}, u32[]{:S(2)}, u32[]{:S(2)}) async-start(f32[4,1,488]{2,1,0:T(1,128)} %reshape.156), calls=%async_computation.3 | async-start | bytes 16384 | tf_op jit(solution)/shard_map/all_to_all | solution.py:68
  20.1 0.7 reshape.158
  20.7 2.7 %gather_fusion.2 = f32[32,61,61]{2,0,1:T(8,128)S(1)} fusion(f32[64,61,61]{2,0,1:T(8,128)S(1)} %copy-done, s32[1024]{0:T(1024)S(1)} %pad_clamp_fusion.1), kind=kCustom, calls=%fused_computation.2 | custom fusion | bytes 952704 | tf_op jit(solution)/shard_map/gather | solution.py:61
  23.5 5.3 %gather_fusion = f32[32,61,61]{2,0,1:T(8,128)} fusion(f32[64,61,61]{2,0,1:T(8,128)} %param.13, s32[1024]{0:T(1024)S(1)} %pad_clamp_fusion.1), kind=kCustom, calls=%fused_computation | custom fusion | bytes 952704 | tf_op jit(solution)/shard_map/gather | solution.py:60
  28.8 3.4 %all-to-all-start.1 = ((f32[4,1,488]{2,1,0:T(1,128)}), f32[4,1,488]{2,1,0:T(1,128)S(1)}, u32[]{:S(2)}, u32[]{:S(2)}) async-start(f32[4,1,488]{2,1,0:T(1,128)} %reshape.158), calls=%async_computation.1 | async-start | bytes 16384 | tf_op jit(solution)/shard_map/all_to_all | solution.py:69
  32.2 2.8 %copy_multiply_fusion.5 = (f32[4,8,61,61]{3,1,2,0:T(8,128)}, f32[4,8,61,61]{3,1,2,0:T(8,128)}) fusion(f32[4,8]{1,0:T(4,128)S(1)} %bitcast_convert_fusion, f32[32,61,61]{2,0,1:T(8,128)S(1)} %gather_fusion.2, f32[32,61,61]{2,0,1:T(8,128)} %gather_fusion), kind=kLoop, calls=%fused_computation.16 | loop fusion | flops 238144 | bytes 1905280 | tf_op jit(solution)/shard_map/mul | solution.py:60
  35.0 3.2 %reshape.160 = f32[4,1,29768]{2,1,0:T(1,128)} reshape(f32[4,61,8,61]{3,2,1,0:T(8,128)} %bitcast.46) | data formatting | bytes 952576
  38.2 3.5 %all-to-all-start = ((f32[4,1,29768]{2,1,0:T(1,128)}), f32[4,1,29768]{2,1,0:T(1,128)S(1)}, u32[]{:S(2)}, u32[]{:S(2)}) async-start(f32[4,1,29768]{2,1,0:T(1,128)} %reshape.160), calls=%async_computation | async-start | bytes 954368 | tf_op jit(solution)/shard_map/all_to_all | solution.py:66
  41.7 3.1 %reshape.154 = f32[4,1,29768]{2,1,0:T(1,128)} reshape(f32[4,61,8,61]{3,2,1,0:T(8,128)} %bitcast.45) | data formatting | bytes 952576
  44.8 0.7 gather_fusion.5
  45.5 0.5 broadcast.86
  46.0 0.7 reduce.1
  46.7 0.1 reshape.157
  46.8 0.7 reduce.3
  47.5 0.1 reshape.159
  47.6 0.6 reduce_sum.100
  48.2 0.1 multiply_bitcast_fusion
  48.3 1.7 %all-to-all-done = f32[4,1,29768]{2,1,0:T(1,128)S(1)} async-done(((f32[4,1,29768]{2,1,0:T(1,128)}), f32[4,1,29768]{2,1,0:T(1,128)S(1)}, u32[]{:S(2)}, u32[]{:S(2)}) %all-to-all-start) | async-done | bytes 476320 | tf_op jit(solution)/shard_map/all_to_all | solution.py:66
  49.9 4.3 %all-to-all-start.2 = ((f32[4,1,29768]{2,1,0:T(1,128)}), f32[4,1,29768]{2,1,0:T(1,128)}, u32[]{:S(2)}, u32[]{:S(2)}) async-start(f32[4,1,29768]{2,1,0:T(1,128)} %reshape.154), calls=%async_computation.2 | async-start | bytes 954368 | tf_op jit(solution)/shard_map/all_to_all | solution.py:67
  54.2 0.1 multiply_exponential_fusion
  54.3 2.1 %reduce.4 = f32[4,29768]{1,0:T(4,128)S(1)} reduce(f32[4,1,29768]{2,1,0:T(1,128)S(1)} %all-to-all-done, f32[]{:T(128)} %broadcast.86), dimensions={1}, to_apply=%all_to_all.18.reduce_sub_computation | reduce | bytes 952580 | tf_op jit(solution)/shard_map/all_to_all | solution.py:66
  56.4 0.6 reshape.161
  57.0 0.8 bitcast_reduce_fusion
  57.7 4.7 %all-to-all-done.2 = f32[4,1,29768]{2,1,0:T(1,128)} async-done(((f32[4,1,29768]{2,1,0:T(1,128)}), f32[4,1,29768]{2,1,0:T(1,128)}, u32[]{:S(2)}, u32[]{:S(2)}) %all-to-all-start.2) | async-done | bytes 476320 | tf_op jit(solution)/shard_map/all_to_all | solution.py:67
  62.4 2.9 %reduce.2 = f32[4,29768]{1,0:T(4,128)S(1)} reduce(f32[4,1,29768]{2,1,0:T(1,128)} %all-to-all-done.2, f32[]{:T(128)} %broadcast.86), dimensions={1}, to_apply=%all_to_all.20.reduce_sub_computation | reduce | bytes 952580 | tf_op jit(solution)/shard_map/all_to_all | solution.py:67
  65.3 0.6 reshape.155
  65.9 0.1 bitcast_reduce_fusion.1
  66.0 6.8 %fusion = f32[8,61,16,128]{3,1,2,0:T(8,128)S(1)} fusion(f32[16,61,8,128]{3,2,1,0:T(8,128)} %bitcast.44, f32[8,61,61,1]{2,0,1,3:T(8,128)S(1)} %bitcast.47), kind=kOutput, calls=%fused_computation.8 | convolution fusion | flops 731578368 | bytes 8114464 | tf_op jit(solution)/shard_map/nkj,bjnl->bknl/dot_general | solution.py:12
  72.9 6.4 %multiply_reduce_fusion.1 = (f32[16,8,128]{2,0,1:T(8,128)S(1)}, f32[16,8,128]{2,0,1:T(8,128)S(1)}, f32[16,8,128]{2,0,1:T(8,128)S(1)}) fusion(f32[61,8]{0,1:T(8,128)S(1)} %copy-done.4, f32[16,61,8]{1,0,2:T(8,128)S(1)} %multiply_exponential_fusion, f32[8,61,16,128]{3,1,2,0:T(8,128)S(1)} %fusion, f32[16,61,8,128]{3,2,1,0:T(8,128)S(1)} %bitcast.57, ...), kind=kOutput, calls=%fused_computation.13 | convolution fusion | flops 739524608 | bytes 8346208 | tf_op jit(solution)/shard_map/binl,nik->bknl/dot_general | solution.py:11
  79.3 0.1 multiply_reduce_fusion.3
  79.5 0.2 fusion.6
  79.7 39.9 %psum.7 = f32[2,16,256]{2,1,0:T(8,128)S(1)} all-reduce(f32[2,16,256]{2,1,0:T(8,128)S(1)} %fusion.6), channel_id=1, replica_groups=mesh['site'=8,'dom'=4] {'site','dom'}, use_global_device_ids=true, to_apply=%region_10.11 | all-reduce | flops 8192 | bytes 65536 | tf_op jit(solution)/shard_map/psum | solution.py:85
  119.6 0.1 reduce_sum.109
  119.7 0.7 constant_dynamic-slice_fusion
  120.4 0.6 scatter_fusion
  121.1 0.7 copy.45
  (44 shorter events, 0.2 us)
Async XLA Ops:
  0.6 20.1 %copy-start = (f32[64,61,61]{2,0,1:T(8,128)S(1)}, f32[64,61,61]{2,0,1:T(8,128)}, u32[]{:S(2)}) copy-start(f32[64,61,61]{2,0,1:T(8,128)} %param.14) | copy-start | bytes 2857732
  9.9 6.9 %all-to-all-start.4 = ((f32[4,1,8]{2,1,0:T(1,128)}), f32[4,1,8]{2,1,0:T(1,128)S(1)}, u32[]{:S(2)}, u32[]{:S(2)}) async-start(f32[4,1,8]{2,1,0:T(1,128)} %bitcast.14), calls=%async_computation.4 | async-start | bytes 4096 | tf_op jit(solution)/shard_map/all_to_all | solution.py:70
  16.8 12.0 %all-to-all-start.3 = ((f32[4,1,488]{2,1,0:T(1,128)}), f32[4,1,488]{2,1,0:T(1,128)S(1)}, u32[]{:S(2)}, u32[]{:S(2)}) async-start(f32[4,1,488]{2,1,0:T(1,128)} %reshape.156), calls=%async_computation.3 | async-start | bytes 16384 | tf_op jit(solution)/shard_map/all_to_all | solution.py:68
  28.8 12.9 %copy-start.13 = (s32[16]{0:T(128)S(1)}, s32[16]{0:T(128)}, u32[]{:S(2)}) copy-start(s32[16]{0:T(128)} %param.21) | copy-start | bytes 196
  28.8 12.9 %copy-start.7 = (s32[1,1024]{1,0:T(1,128)S(1)}, s32[1,1024]{1,0:T(1,128)}, u32[]{:S(2)}) copy-start(s32[1,1024]{1,0:T(1,128)} %param.19) | copy-start | bytes 12292
  28.8 9.4 %all-to-all-start.1 = ((f32[4,1,488]{2,1,0:T(1,128)}), f32[4,1,488]{2,1,0:T(1,128)S(1)}, u32[]{:S(2)}, u32[]{:S(2)}) async-start(f32[4,1,488]{2,1,0:T(1,128)} %reshape.158), calls=%async_computation.1 | async-start | bytes 16384 | tf_op jit(solution)/shard_map/all_to_all | solution.py:69
  38.2 11.8 %all-to-all-start = ((f32[4,1,29768]{2,1,0:T(1,128)}), f32[4,1,29768]{2,1,0:T(1,128)S(1)}, u32[]{:S(2)}, u32[]{:S(2)}) async-start(f32[4,1,29768]{2,1,0:T(1,128)} %reshape.160), calls=%async_computation | async-start | bytes 954368 | tf_op jit(solution)/shard_map/all_to_all | solution.py:66
  41.7 3.2 %copy-start.9 = (s32[16]{0:T(128)}, s32[16]{0:T(128)S(1)}, u32[]{:S(2)}) copy-start(s32[16]{0:T(128)S(1)} %compare_select_fusion.1) | copy-start | bytes 196
  45.5 8.7 %copy-start.5 = (f32[16]{0:T(128)}, f32[16]{0:T(128)S(1)}, u32[]{:S(2)}) copy-start(f32[16]{0:T(128)S(1)} %gather_fusion.5) | copy-start | bytes 196
  48.2 6.1 %copy-start.3 = (f32[61,8]{0,1:T(8,128)}, f32[61,8]{0,1:T(8,128)S(1)}, u32[]{:S(2)}) copy-start(f32[61,8]{0,1:T(8,128)S(1)} %multiply_bitcast_fusion) | copy-start | bytes 5860
  49.9 12.5 %all-to-all-start.2 = ((f32[4,1,29768]{2,1,0:T(1,128)}), f32[4,1,29768]{2,1,0:T(1,128)}, u32[]{:S(2)}, u32[]{:S(2)}) async-start(f32[4,1,29768]{2,1,0:T(1,128)} %reshape.154), calls=%async_computation.2 | async-start | bytes 954368 | tf_op jit(solution)/shard_map/all_to_all | solution.py:67
  66.0 6.9 %copy-start.2 = (f32[8,61,61]{2,0,1:T(8,128)S(1)}, f32[8,61,61]{2,0,1:T(8,128)}, u32[]{:S(2)}) copy-start(f32[8,61,61]{2,0,1:T(8,128)} %bitcast_reduce_fusion) | copy-start | bytes 357220
  66.0 6.9 %copy-start.4 = (f32[61,8]{0,1:T(8,128)S(1)}, f32[61,8]{0,1:T(8,128)}, u32[]{:S(2)}) copy-start(f32[61,8]{0,1:T(8,128)} %copy-done.3) | copy-start | bytes 5860
  66.0 6.9 %copy-start.8 = (f32[8,61]{1,0:T(8,128)S(1)}, f32[8,61]{1,0:T(8,128)}, u32[]{:S(2)}) copy-start(f32[8,61]{1,0:T(8,128)} %reduce_sum.100) | copy-start | bytes 5860
  66.0 6.9 %copy-start.12 = (f32[16,61,1,1024]{3,2,1,0:T(1,128)S(1)}, f32[16,61,1,1024]{3,2,1,0:T(1,128)}, u32[]{:S(2)}) copy-start(f32[16,61,1,1024]{3,2,1,0:T(1,128)} %param.11) | copy-start | bytes 11993092
  72.9 6.6 %copy-start.11 = (s32[1,8]{1,0:T(1,128)S(1)}, s32[1,8]{1,0:T(1,128)}, u32[]{:S(2)}) copy-start(s32[1,8]{1,0:T(1,128)} %param.20) | copy-start | bytes 100
  72.9 47.5 %copy-start.6 = (f32[16]{0:T(128)S(1)}, f32[16]{0:T(128)}, u32[]{:S(2)}) copy-start(f32[16]{0:T(128)} %copy-done.5) | copy-start | bytes 196
  72.9 47.5 %copy-start.10 = (s32[16]{0:T(128)S(1)}, s32[16]{0:T(128)}, u32[]{:S(2)}) copy-start(s32[16]{0:T(128)} %copy-done.9) | copy-start | bytes 196
  121.0 0.8 copy-start.1
where the time goes:
time: 123 us; the launch traced here: 122 us
  blocking collectives  46.1 us (37%)
  local copies, waits for them, and re-layouts  25.3 us (21%)
  starting transfers between devices  17.6 us (14%)
  matrix products  13.5 us (11%)
  other arithmetic  11.7 us (10%)
  waiting for transfers between devices  6.6 us (5%)
    psum x1, blocking collectives, on_device(): everything = lax.psum(part_local, ('site', 'dom'))  39.9 us
    unnamed x38, local copies, waits for them, and re-layouts  10.6 us
    dot_general x1, matrix products, project(): jnp.einsum('nkj,bjnl->bknl', vec_right, lower, precision=lax.Precision.HI...  6.82 us
    dot_general x1, matrix products, project(): jnp.einsum('binl,nik->bknl', scaled, vec_left, precision=lax.Precision.HI...  6.42 us
    all_gather x1, blocking collectives, on_device(): wanted = lax.all_gather(block_partition, 'dom', axis=0, tiled=True)  6.22 us
    gather x1, local copies, waits for them, and re-layouts, on_device(): send_left = left_vectors[clipped] * inside[:, :, None, None]  5.29 us
    all_to_all x1, waiting for transfers between devices, on_device(): lax.all_to_all(send_right, 'dom', split_axis=0, concat_axis=0, tiled=True)  4.67 us
    all_to_all x1, starting transfers between devices, on_device(): lax.all_to_all(send_right, 'dom', split_axis=0, concat_axis=0, tiled=True)  4.3 us
  transfers between devices with their start and end apart: 5, of which 3 were waited for; matrix products, arithmetic and copies ran while one was open for 23% of the time, Pallas kernels for 0%

commit v1 on v0

--- a/solution.py
+++ b/solution.py
@@ -82,7 +82,7 @@
         jnp.float32
     )
     part_local = jnp.einsum("abn,np->abp", sums, onehot, precision=lax.Precision.HIGHEST)
-    everything = lax.psum(part_local, ("site", "dom"))
+    everything = lax.psum(lax.psum(part_local, "dom"), "site")
     share = lax.dynamic_slice_in_dim(everything, lax.axis_index("dom") * owned, owned, 2)
     totals = jnp.sum(everything, axis=2)
     updated = times - totals[0] / totals[1]

time: 123 us -> 131 us (1.065)
  blocking collectives: 46.1 us -> 54.1 us
    psum x1 -> x2, blocking collectives: 39.9 us -> 47.9 us  [on_device(): everything = lax.psum(lax.psum(part_local, 'dom'), 'site')]
  transfers between devices with their start and end apart: 5 -> 5, of which waited for: 3 -> 3; matrix products, arithmetic and copies ran while one was open for 23% -> 22% of each run, Pallas kernels for 0% -> 0%
where the time goes in v1:
time: 131 us; the launch traced here: 130 us
  blocking collectives  54.1 us (41%)
  local copies, waits for them, and re-layouts  25.3 us (19%)
  starting transfers between devices  17.6 us (13%)
  matrix products  13.5 us (10%)
  other arithmetic  11.7 us (9%)
  waiting for transfers between devices  6.6 us (5%)
    psum x2, blocking collectives, on_device(): everything = lax.psum(lax.psum(part_local, 'dom'), 'site')  47.9 us
    unnamed x38, local copies, waits for them, and re-layouts  10.6 us
    dot_general x1, matrix products, project(): jnp.einsum('nkj,bjnl->bknl', vec_right, lower, precision=lax.Precision.HI...  6.82 us
    dot_general x1, matrix products, project(): jnp.einsum('binl,nik->bknl', scaled, vec_left, precision=lax.Precision.HI...  6.42 us
    all_gather x1, blocking collectives, on_device(): wanted = lax.all_gather(block_partition, 'dom', axis=0, tiled=True)  6.22 us
    gather x1, local copies, waits for them, and re-layouts, on_device(): send_left = left_vectors[clipped] * inside[:, :, None, None]  5.29 us
    all_to_all x1, waiting for transfers between devices, on_device(): lax.all_to_all(send_right, 'dom', split_axis=0, concat_axis=0, tiled=True)  4.67 us
    all_to_all x1, starting transfers between devices, on_device(): lax.all_to_all(send_right, 'dom', split_axis=0, concat_axis=0, tiled=True)  4.3 us
  transfers between devices with their start and end apart: 5, of which 3 were waited for; matrix products, arithmetic and copies ran while one was open for 22% of the time, Pallas kernels for 0%

profile of v1, /device:TPU:0, one launch (start us, length us, event | category | flops | bytes accessed | tf_op | source)
XLA Modules:
  0.0 129.8 jit_solution(9390500443762465183)
XLA Ops:
  0.6 0.8 copy.76
  1.5 6.2 %all-gather = s32[4,1,8]{2,1,0:T(1,128)S(1)} all-gather(s32[1,1,8]{2,1,0:T(1,128)} %bitcast.55), channel_id=1, replica_groups=mesh['site'=8,'dom'=4] {'dom'}, dimensions={0}, use_global_device_ids=true | all-gather | bytes 160 | tf_op jit(solution)/shard_map/all_gather | solution.py:56
  7.7 0.1 reshape.73
  7.8 1.4 %gather_fusion.4 = f32[32]{0:T(128)S(1)} fusion(f32[64]{0:T(128)} %param.17, s32[1024]{0:T(1024)S(1)} %pad_clamp_fusion.1), kind=kCustom, calls=%fused_computation.4 | custom fusion | bytes 384 | tf_op jit(solution)/shard_map/gather | solution.py:64
  9.2 0.1 reshape.104
  9.3 0.6 bitcast_select_fusion
  9.9 3.2 %all-to-all-start.4 = ((f32[4,1,8]{2,1,0:T(1,128)}), f32[4,1,8]{2,1,0:T(1,128)S(1)}, u32[]{:S(2)}, u32[]{:S(2)}) async-start(f32[4,1,8]{2,1,0:T(1,128)} %bitcast.14), calls=%async_computation.4 | async-start | bytes 4096 | tf_op jit(solution)/shard_map/all_to_all | solution.py:70
  13.1 1.3 %gather_fusion.3 = f32[32,61]{1,0:T(8,128)S(1)} fusion(f32[64,61]{1,0:T(8,128)} %param.15, s32[1024]{0:T(1024)S(1)} %pad_clamp_fusion.1), kind=kCustom, calls=%fused_computation.3 | custom fusion | bytes 15744 | tf_op jit(solution)/shard_map/gather | solution.py:62
  14.4 1.3 %gather_fusion.1 = f32[32,61]{1,0:T(8,128)S(1)} fusion(f32[64,61]{1,0:T(8,128)} %param.16, s32[1024]{0:T(1024)S(1)} %pad_clamp_fusion.1), kind=kCustom, calls=%fused_computation.1 | custom fusion | bytes 15744 | tf_op jit(solution)/shard_map/gather | solution.py:63
  15.8 0.1 bitcast_multiply_fusion.2
  15.8 0.7 reshape.156
  16.5 0.3 all-to-all-done.4
  16.8 3.2 %all-to-all-start.3 = ((f32[4,1,488]{2,1,0:T(1,128)}), f32[4,1,488]{2,1,0:T(1,128)S(1)}, u32[]{:S(2)}, u32[]{:S(2)}) async-start(f32[4,1,488]{2,1,0:T(1,128)} %reshape.156), calls=%async_computation.3 | async-start | bytes 16384 | tf_op jit(solution)/shard_map/all_to_all | solution.py:68
  20.1 0.7 reshape.158
  20.7 2.7 %gather_fusion.2 = f32[32,61,61]{2,0,1:T(8,128)S(1)} fusion(f32[64,61,61]{2,0,1:T(8,128)S(1)} %copy-done, s32[1024]{0:T(1024)S(1)} %pad_clamp_fusion.1), kind=kCustom, calls=%fused_computation.2 | custom fusion | bytes 952704 | tf_op jit(solution)/shard_map/gather | solution.py:61
  23.5 5.3 %gather_fusion = f32[32,61,61]{2,0,1:T(8,128)} fusion(f32[64,61,61]{2,0,1:T(8,128)} %param.13, s32[1024]{0:T(1024)S(1)} %pad_clamp_fusion.1), kind=kCustom, calls=%fused_computation | custom fusion | bytes 952704 | tf_op jit(solution)/shard_map/gather | solution.py:60
  28.8 3.4 %all-to-all-start.1 = ((f32[4,1,488]{2,1,0:T(1,128)}), f32[4,1,488]{2,1,0:T(1,128)S(1)}, u32[]{:S(2)}, u32[]{:S(2)}) async-start(f32[4,1,488]{2,1,0:T(1,128)} %reshape.158), calls=%async_computation.1 | async-start | bytes 16384 | tf_op jit(solution)/shard_map/all_to_all | solution.py:69
  32.2 2.8 %copy_multiply_fusion.5 = (f32[4,8,61,61]{3,1,2,0:T(8,128)}, f32[4,8,61,61]{3,1,2,0:T(8,128)}) fusion(f32[4,8]{1,0:T(4,128)S(1)} %bitcast_convert_fusion, f32[32,61,61]{2,0,1:T(8,128)S(1)} %gather_fusion.2, f32[32,61,61]{2,0,1:T(8,128)} %gather_fusion), kind=kLoop, calls=%fused_computation.16 | loop fusion | flops 238144 | bytes 1905280 | tf_op jit(solution)/shard_map/mul | solution.py:60
  35.0 3.2 %reshape.160 = f32[4,1,29768]{2,1,0:T(1,128)} reshape(f32[4,61,8,61]{3,2,1,0:T(8,128)} %bitcast.46) | data formatting | bytes 952576
  38.2 3.5 %all-to-all-start = ((f32[4,1,29768]{2,1,0:T(1,128)}), f32[4,1,29768]{2,1,0:T(1,128)S(1)}, u32[]{:S(2)}, u32[]{:S(2)}) async-start(f32[4,1,29768]{2,1,0:T(1,128)} %reshape.160), calls=%async_computation | async-start | bytes 954368 | tf_op jit(solution)/shard_map/all_to_all | solution.py:66
  41.7 3.1 %reshape.154 = f32[4,1,29768]{2,1,0:T(1,128)} reshape(f32[4,61,8,61]{3,2,1,0:T(8,128)} %bitcast.45) | data formatting | bytes 952576
  44.8 0.7 gather_fusion.5
  45.5 0.5 broadcast.86
  46.0 0.7 reduce.1
  46.7 0.1 reshape.157
  46.8 0.7 reduce.3
  47.5 0.1 reshape.159
  47.6 0.6 reduce_sum.100
  48.2 0.1 multiply_bitcast_fusion
  48.3 1.7 %all-to-all-done = f32[4,1,29768]{2,1,0:T(1,128)S(1)} async-done(((f32[4,1,29768]{2,1,0:T(1,128)}), f32[4,1,29768]{2,1,0:T(1,128)S(1)}, u32[]{:S(2)}, u32[]{:S(2)}) %all-to-all-start) | async-done | bytes 476320 | tf_op jit(solution)/shard_map/all_to_all | solution.py:66
  49.9 4.3 %all-to-all-start.2 = ((f32[4,1,29768]{2,1,0:T(1,128)}), f32[4,1,29768]{2,1,0:T(1,128)}, u32[]{:S(2)}, u32[]{:S(2)}) async-start(f32[4,1,29768]{2,1,0:T(1,128)} %reshape.154), calls=%async_computation.2 | async-start | bytes 954368 | tf_op jit(solution)/shard_map/all_to_all | solution.py:67
  54.2 0.1 multiply_exponential_fusion
  54.3 2.1 %reduce.4 = f32[4,29768]{1,0:T(4,128)S(1)} reduce(f32[4,1,29768]{2,1,0:T(1,128)S(1)} %all-to-all-done, f32[]{:T(128)} %broadcast.86), dimensions={1}, to_apply=%all_to_all.18.reduce_sub_computation | reduce | bytes 952580 | tf_op jit(solution)/shard_map/all_to_all | solution.py:66
  56.4 0.6 reshape.161
  57.0 0.8 bitcast_reduce_fusion
  57.7 4.7 %all-to-all-done.2 = f32[4,1,29768]{2,1,0:T(1,128)} async-done(((f32[4,1,29768]{2,1,0:T(1,128)}), f32[4,1,29768]{2,1,0:T(1,128)}, u32[]{:S(2)}, u32[]{:S(2)}) %all-to-all-start.2) | async-done | bytes 476320 | tf_op jit(solution)/shard_map/all_to_all | solution.py:67
  62.4 2.9 %reduce.2 = f32[4,29768]{1,0:T(4,128)S(1)} reduce(f32[4,1,29768]{2,1,0:T(1,128)} %all-to-all-done.2, f32[]{:T(128)} %broadcast.86), dimensions={1}, to_apply=%all_to_all.20.reduce_sub_computation | reduce | bytes 952580 | tf_op jit(solution)/shard_map/all_to_all | solution.py:67
  65.3 0.6 reshape.155
  66.0 6.8 %fusion = f32[8,61,16,128]{3,1,2,0:T(8,128)S(1)} fusion(f32[16,61,8,128]{3,2,1,0:T(8,128)} %bitcast.44, f32[8,61,61,1]{2,0,1,3:T(8,128)S(1)} %bitcast.47), kind=kOutput, calls=%fused_computation.8 | convolution fusion | flops 731578368 | bytes 8114464 | tf_op jit(solution)/shard_map/nkj,bjnl->bknl/dot_general | solution.py:12
  72.9 6.4 %multiply_reduce_fusion.1 = (f32[16,8,128]{2,0,1:T(8,128)S(1)}, f32[16,8,128]{2,0,1:T(8,128)S(1)}, f32[16,8,128]{2,0,1:T(8,128)S(1)}) fusion(f32[61,8]{0,1:T(8,128)S(1)} %copy-done.4, f32[16,61,8]{1,0,2:T(8,128)S(1)} %multiply_exponential_fusion, f32[8,61,16,128]{3,1,2,0:T(8,128)S(1)} %fusion, f32[16,61,8,128]{3,2,1,0:T(8,128)S(1)} %bitcast.57, ...), kind=kOutput, calls=%fused_computation.13 | convolution fusion | flops 739524608 | bytes 8346208 | tf_op jit(solution)/shard_map/binl,nik->bknl/dot_general | solution.py:11
  79.3 0.1 multiply_reduce_fusion.3
  79.5 0.2 fusion.6
  79.7 10.3 %psum.14 = f32[2,16,256]{2,1,0:T(8,128)S(1)} all-reduce(f32[2,16,256]{2,1,0:T(8,128)S(1)} %fusion.6), channel_id=1, replica_groups=mesh['site'=8,'dom'=4] {'dom'}, use_global_device_ids=true, to_apply=%region_10.11 | all-reduce | flops 8192 | bytes 65536 | tf_op jit(solution)/shard_map/psum | solution.py:85
  90.0 37.6 %psum.15 = f32[2,16,256]{2,1,0:T(8,128)S(1)} all-reduce(f32[2,16,256]{2,1,0:T(8,128)S(1)} %psum.14), channel_id=1, replica_groups=mesh['site'=8,'dom'=4] {'site'}, use_global_device_ids=true, to_apply=%region_11.12 | all-reduce | flops 8192 | bytes 65536 | tf_op jit(solution)/shard_map/psum | solution.py:85
  127.6 0.1 reduce_sum.109
  127.7 0.7 constant_dynamic-slice_fusion
  128.4 0.6 scatter_fusion
  129.1 0.7 copy.45
  (45 shorter events, 0.3 us)
Async XLA Ops:
  0.6 20.1 %copy-start = (f32[64,61,61]{2,0,1:T(8,128)S(1)}, f32[64,61,61]{2,0,1:T(8,128)}, u32[]{:S(2)}) copy-start(f32[64,61,61]{2,0,1:T(8,128)} %param.14) | copy-start | bytes 2857732
  9.9 6.9 %all-to-all-start.4 = ((f32[4,1,8]{2,1,0:T(1,128)}), f32[4,1,8]{2,1,0:T(1,128)S(1)}, u32[]{:S(2)}, u32[]{:S(2)}) async-start(f32[4,1,8]{2,1,0:T(1,128)} %bitcast.14), calls=%async_computation.4 | async-start | bytes 4096 | tf_op jit(solution)/shard_map/all_to_all | solution.py:70
  16.8 12.0 %all-to-all-start.3 = ((f32[4,1,488]{2,1,0:T(1,128)}), f32[4,1,488]{2,1,0:T(1,128)S(1)}, u32[]{:S(2)}, u32[]{:S(2)}) async-start(f32[4,1,488]{2,1,0:T(1,128)} %reshape.156), calls=%async_computation.3 | async-start | bytes 16384 | tf_op jit(solution)/shard_map/all_to_all | solution.py:68
  28.8 12.9 %copy-start.13 = (s32[16]{0:T(128)S(1)}, s32[16]{0:T(128)}, u32[]{:S(2)}) copy-start(s32[16]{0:T(128)} %param.21) | copy-start | bytes 196
  28.8 12.9 %copy-start.7 = (s32[1,1024]{1,0:T(1,128)S(1)}, s32[1,1024]{1,0:T(1,128)}, u32[]{:S(2)}) copy-start(s32[1,1024]{1,0:T(1,128)} %param.19) | copy-start | bytes 12292
  28.8 9.4 %all-to-all-start.1 = ((f32[4,1,488]{2,1,0:T(1,128)}), f32[4,1,488]{2,1,0:T(1,128)S(1)}, u32[]{:S(2)}, u32[]{:S(2)}) async-start(f32[4,1,488]{2,1,0:T(1,128)} %reshape.158), calls=%async_computation.1 | async-start | bytes 16384 | tf_op jit(solution)/shard_map/all_to_all | solution.py:69
  38.2 11.8 %all-to-all-start = ((f32[4,1,29768]{2,1,0:T(1,128)}), f32[4,1,29768]{2,1,0:T(1,128)S(1)}, u32[]{:S(2)}, u32[]{:S(2)}) async-start(f32[4,1,29768]{2,1,0:T(1,128)} %reshape.160), calls=%async_computation | async-start | bytes 954368 | tf_op jit(solution)/shard_map/all_to_all | solution.py:66
  41.7 3.2 %copy-start.9 = (s32[16]{0:T(128)}, s32[16]{0:T(128)S(1)}, u32[]{:S(2)}) copy-start(s32[16]{0:T(128)S(1)} %compare_select_fusion.1) | copy-start | bytes 196
  45.5 8.7 %copy-start.5 = (f32[16]{0:T(128)}, f32[16]{0:T(128)S(1)}, u32[]{:S(2)}) copy-start(f32[16]{0:T(128)S(1)} %gather_fusion.5) | copy-start | bytes 196
  48.2 6.1 %copy-start.3 = (f32[61,8]{0,1:T(8,128)}, f32[61,8]{0,1:T(8,128)S(1)}, u32[]{:S(2)}) copy-start(f32[61,8]{0,1:T(8,128)S(1)} %multiply_bitcast_fusion) | copy-start | bytes 5860
  49.9 12.5 %all-to-all-start.2 = ((f32[4,1,29768]{2,1,0:T(1,128)}), f32[4,1,29768]{2,1,0:T(1,128)}, u32[]{:S(2)}, u32[]{:S(2)}) async-start(f32[4,1,29768]{2,1,0:T(1,128)} %reshape.154), calls=%async_computation.2 | async-start | bytes 954368 | tf_op jit(solution)/shard_map/all_to_all | solution.py:67
  66.0 6.9 %copy-start.2 = (f32[8,61,61]{2,0,1:T(8,128)S(1)}, f32[8,61,61]{2,0,1:T(8,128)}, u32[]{:S(2)}) copy-start(f32[8,61,61]{2,0,1:T(8,128)} %bitcast_reduce_fusion) | copy-start | bytes 357220
  66.0 6.9 %copy-start.4 = (f32[61,8]{0,1:T(8,128)S(1)}, f32[61,8]{0,1:T(8,128)}, u32[]{:S(2)}) copy-start(f32[61,8]{0,1:T(8,128)} %copy-done.3) | copy-start | bytes 5860
  66.0 6.9 %copy-start.8 = (f32[8,61]{1,0:T(8,128)S(1)}, f32[8,61]{1,0:T(8,128)}, u32[]{:S(2)}) copy-start(f32[8,61]{1,0:T(8,128)} %reduce_sum.100) | copy-start | bytes 5860
  66.0 6.9 %copy-start.12 = (f32[16,61,1,1024]{3,2,1,0:T(1,128)S(1)}, f32[16,61,1,1024]{3,2,1,0:T(1,128)}, u32[]{:S(2)}) copy-start(f32[16,61,1,1024]{3,2,1,0:T(1,128)} %param.11) | copy-start | bytes 11993092
  72.9 6.6 %copy-start.11 = (s32[1,8]{1,0:T(1,128)S(1)}, s32[1,8]{1,0:T(1,128)}, u32[]{:S(2)}) copy-start(s32[1,8]{1,0:T(1,128)} %param.20) | copy-start | bytes 100
  72.9 55.5 %copy-start.6 = (f32[16]{0:T(128)S(1)}, f32[16]{0:T(128)}, u32[]{:S(2)}) copy-start(f32[16]{0:T(128)} %copy-done.5) | copy-start | bytes 196
  72.9 55.5 %copy-start.10 = (s32[16]{0:T(128)S(1)}, s32[16]{0:T(128)}, u32[]{:S(2)}) copy-start(s32[16]{0:T(128)} %copy-done.9) | copy-start | bytes 196
  129.1 0.8 copy-start.1
